TPU v7x, 32 devices: a whole 2x2x4 slice. The times are simulated.
32 devices in a mesh: seq: 16 (over z, x, core), chan: 2 (over y).
Axes of the slice: x: 2, y: 2, z: 4, core: 2. Of those that a mesh axis runs over, the one named last changes fastest.
Arguments:
- signal: bfloat16 [524288, 256], P('seq', 'chan'), parts along dimension 1, may hold values from -6 to 6
- gate_values: bfloat16 [524288, 256], P('seq', 'chan'), parts along dimension 1, may hold values from -4 to 4
- skip_gain: float32 [256], P('chan'), parts along dimension 0, may hold values from 0.25 to 2
- filter_spectrum: bfloat16 [2, 512, 1024, 256], P(None, 'seq', None, 'chan'), parts along dimension 3, may hold values from -4 to 4, as said below
Outputs:
- gated_output: bfloat16 [524288, 256], P('seq', 'chan'), parts along dimension 1
There are 2 independent parts, one for each index of `chan`. A program takes and returns all parts, laid end to end along the dimension named above; each array names one. Nothing has to cross between parts.
Inputs may be any that keep to these rules, and one draw needn't show every extreme that they name: `filter_spectrum`: the spectrum of a real filter: the complex entry at frequency k equals the conjugate of the entry at frequency (524288 - k) mod 524288.
All inputs are finite; a program needn't handle non-finite values.
Results may differ from a plain program's by a relative error of at most 0.0085.
Values may be sent and summed in bfloat16 or wider, within the bound.
A program may use at most 256 MiB of HBM per device.

v0:
```python
import math

import jax
import jax.numpy as jnp
from jax import lax
from jax.sharding import PartitionSpec as P

OUTER = 1024
INNER = 512
SEQ = 524288


def tables(length):
    indices = lax.iota(jnp.int32, length)
    angles = (
        2.0 * math.pi / length * (indices[:, None] * indices[None, :] % length).astype(jnp.float32)
    )
    return (jnp.cos(angles).astype(jnp.bfloat16), jnp.sin(angles).astype(jnp.bfloat16))


def twiddle(c_values, b_values, length):
    angles = (
        2.0
        * math.pi
        / length
        * (c_values[:, None] * b_values[None, :] % length).astype(jnp.float32)
    )
    return (jnp.cos(angles), jnp.sin(angles))


def spectral_product(spectrum, filter_cols):
    spec_re = spectrum[0].astype(jnp.float32)
    spec_im = spectrum[1].astype(jnp.float32)
    filter_re = filter_cols[0].astype(jnp.float32)
    filter_im = filter_cols[1].astype(jnp.float32)
    return jnp.stack(
        [spec_re * filter_re - spec_im * filter_im, spec_re * filter_im + spec_im * filter_re]
    ).astype(jnp.bfloat16)


def local(signal, gate_values, skip_gain, filter_spectrum):
    shards = lax.axis_size("seq")
    own_index = lax.axis_index("seq")
    channels = signal.shape[1]
    outer_loc = OUTER // shards
    inner_loc = INNER // shards
    cos_a, sin_a = tables(OUTER)
    cos_b, sin_b = tables(INNER)
    inner_table = jnp.stack([cos_b, sin_b])
    outer_scale = 1.0 / math.sqrt(OUTER)
    inner_scale = 1.0 / math.sqrt(INNER)
    own_b = own_index * inner_loc + lax.iota(jnp.int32, inner_loc)
    own_c = own_index * outer_loc + lax.iota(jnp.int32, outer_loc)
    cols_cos, cols_sin = twiddle(lax.iota(jnp.int32, OUTER), own_b, SEQ)
    rows_cos, rows_sin = twiddle(own_c, lax.iota(jnp.int32, INNER), SEQ)
    cols_cos = cols_cos[:, :, None]
    cols_sin = cols_sin[:, :, None]
    rows_cos = rows_cos[:, :, None]
    rows_sin = rows_sin[:, :, None]
    signal_grid = signal.reshape(outer_loc, INNER, channels)
    pieces = lax.all_to_all(signal_grid, "seq", split_axis=1, concat_axis=0, tiled=True)
    breadth = pieces.shape[2]
    flattened = pieces.reshape(OUTER, inner_loc * breadth)
    fwd_re = jnp.dot(cos_a, flattened, preferred_element_type=jnp.float32).reshape(
        OUTER, inner_loc, breadth
    )
    fwd_im = -jnp.dot(sin_a, flattened, preferred_element_type=jnp.float32).reshape(
        OUTER, inner_loc, breadth
    )
    columns = jnp.stack(
        [
            (fwd_re * cols_cos + fwd_im * cols_sin) * outer_scale,
            (fwd_im * cols_cos - fwd_re * cols_sin) * outer_scale,
        ]
    ).astype(jnp.bfloat16)
    partials = jnp.einsum(
        "tdb,scbk->tscdk",
        inner_table,
        lax.all_to_all(columns, "seq", split_axis=1, concat_axis=2, tiled=True),
        preferred_element_type=jnp.float32,
    )
    spectrum = jnp.stack(
        [
            (partials[0, 0] + partials[1, 1]) * inner_scale,
            (partials[0, 1] - partials[1, 0]) * inner_scale,
        ]
    ).astype(jnp.bfloat16)
    filter_cols = lax.all_to_all(filter_spectrum, "seq", split_axis=2, concat_axis=1, tiled=True)
    product = spectral_product(spectrum, jnp.swapaxes(filter_cols, 1, 2))
    partials = jnp.einsum(
        "tbd,scdk->tscbk", inner_table, product, preferred_element_type=jnp.float32
    )
    back_re = (partials[0, 0] - partials[1, 1]) * inner_scale
    back_im = (partials[0, 1] + partials[1, 0]) * inner_scale
    rotated = jnp.stack(
        [back_re * rows_cos - back_im * rows_sin, back_re * rows_sin + back_im * rows_cos]
    ).astype(jnp.bfloat16)
    pieces = lax.all_to_all(rotated, "seq", split_axis=2, concat_axis=1, tiled=True)
    breadth = pieces.shape[3]
    convolved = (
        jnp.dot(
            cos_a, pieces[0].reshape(OUTER, inner_loc * breadth), preferred_element_type=jnp.float32
        )
        - jnp.dot(
            sin_a, pieces[1].reshape(OUTER, inner_loc * breadth), preferred_element_type=jnp.float32
        )
    ) * outer_scale
    by_columns = convolved.reshape(OUTER, inner_loc, breadth).astype(jnp.bfloat16)
    convolved = lax.all_to_all(by_columns, "seq", split_axis=0, concat_axis=1, tiled=True).reshape(
        outer_loc * INNER, channels
    )
    result = gate_values.astype(jnp.float32) * (
        convolved.astype(jnp.float32) + skip_gain[None, :] * signal.astype(jnp.float32)
    )
    return result.astype(jnp.bfloat16)


def solution(mesh):
    return jax.shard_map(
        local,
        mesh=mesh,
        in_specs=(P("seq", "chan"), P("seq", "chan"), P("chan"), P(None, "seq", None, "chan")),
        out_specs=P("seq", "chan"),
        check_vma=False,
    )
```

profile of v0, /device:TPU:11, one launch (start us, length us, event | category | flops | bytes accessed | tf_op | source)
XLA Modules:
  0.0 1841.8 jit_solution(5718546721229991774)
XLA Ops:
  18.7 18.6 %copy.71 = bf16[2,32,1024,128]{3,1,0,2:T(8,128)(2,1)} copy(bf16[2,32,1024,128]{3,2,1,0:T(8,128)(2,1)} %param.7) | data formatting | bytes 33554432 | tf_op args[3]
  37.3 163.8 %all-to-all-done = bf16[64,512,128]{2,0,1:T(8,128)(2,1)} async-done(((bf16[64,512,128]{2,0,1:T(8,128)(2,1)}), bf16[64,512,128]{2,0,1:T(8,128)(2,1)}, u32[]{:S(2)}, u32[]{:S(2)}) %all-to-all-start) | async-done | bytes 8388640 | tf_op jit(solution)/shard_map/all_to_all | solution.py:61
  206.7 15.7 fusion.88
  236.3 15.3 copy.108
  263.5 30.3 %fusion.35 = f32[1024,32,128]{2,0,1:T(8,128)} fusion(bf16[32,128,1024]{2,1,0:T(8,128)(2,1)} %bitcast.161), kind=kOutput, calls=%fused_computation.60 | convolution fusion | flops 8605663232 | bytes 25165824 | tf_op jit(solution)/shard_map/dot_general | solution.py:67
  293.8 19.3 %fusion.16 = (bf16[1,1024,32,128]{3,1,2,0:T(8,128)(2,1)S(1)}, bf16[1,1024,32,128]{3,1,2,0:T(8,128)(2,1)}) fusion(f32[1024,32,128]{2,0,1:T(8,128)} %fusion.35, f32[1024,32]{0,1:T(8,128)S(1)} %get-tuple-element.15, f32[1024,32]{0,1:T(8,128)S(1)} %get-tuple-element.14, bf16[32,128,1024]{2,1,0:T(8,128)(2,1)S(1)} %bitcast.162, bf16[1024,1024,1]{1,0,2:T(8,128)(2,1)S(1)} %fusion.88), kind=kOutput, calls=%fused_computation.37 | convolution fusion | flops 8636071936 | bytes 44302336 | tf_op jit(solution)/shard_map/dot_general | solution.py:64
  319.3 40.3 %copy.65 = bf16[2,1024,32,128]{3,2,0,1:T(8,128)(2,1)} copy(bf16[2,1024,32,128]{3,1,2,0:T(8,128)(2,1)S(1)} %pad_maximum_fusion) | data formatting | bytes 33554432 | tf_op jit(solution)/shard_map/stack | solution.py:70
  359.6 208.4 %all-to-all-done.2 = bf16[2,32,1024,128]{3,1,0,2:T(8,128)(2,1)} async-done(((bf16[2,32,1024,128]{3,1,0,2:T(8,128)(2,1)}), bf16[2,32,1024,128]{3,1,0,2:T(8,128)(2,1)}, u32[]{:S(2)}, u32[]{:S(2)}) %all-to-all-start.2) | async-done | bytes 16777248 | tf_op jit(solution)/shard_map/all_to_all | solution.py:88
  578.1 17.8 copy.73
  596.0 23.9 %copy.74 = bf16[2,512,64,128]{1,3,2,0:T(8,128)(2,1)} copy(bf16[2,512,64,128]{3,2,1,0:T(8,128)(2,1)} %bitcast.154) | data formatting | bytes 33554432 | tf_op jit(solution)/shard_map/all_to_all | solution.py:88
  619.8 315.2 %all-to-all-done.1 = bf16[2,1024,32,128]{3,2,0,1:T(8,128)(2,1)} async-done(((bf16[2,1024,32,128]{3,2,0,1:T(8,128)(2,1)}), bf16[2,1024,32,128]{3,2,0,1:T(8,128)(2,1)}, u32[]{:S(2)}, u32[]{:S(2)}) %all-to-all-start.1) | async-done | bytes 16777248 | tf_op jit(solution)/shard_map/all_to_all | solution.py:79
  935.0 15.3 copy.67
  950.3 31.7 %convolution_bitcast_fusion.1 = f32[2,2,64,512,128]{3,4,0,2,1:T(8,128)} fusion(bf16[2,64,512,128,1]{3,2,4,1,0:T(8,128)(2,1)} %bitcast.160, bf16[1,512,512]{2,1,0:T(8,128)(2,1)S(1)} %get-tuple-element.18, bf16[1,512,512]{2,1,0:T(8,128)(2,1)S(1)} %get-tuple-element.19), kind=kOutput, calls=%fused_computation.1 | convolution fusion | flops 17181966336 | bytes 84934656 | tf_op jit(solution)/shard_map/tdb,scbk->tscdk/dot_general | solution.py:76
  982.0 36.8 %fusion.1 = (bf16[1,64,512,128]{2,3,1,0:T(8,128)(2,1)}, bf16[1,64,512,128]{2,3,1,0:T(8,128)(2,1)}, bf16[1,64,512,128]{2,3,1,0:T(8,128)(2,1)}) fusion(bf16[2,64,512,128]{2,3,1,0:T(8,128)(2,1)} %bitcast.151, f32[2,2,64,512,128]{3,4,0,2,1:T(8,128)} %convolution_bitcast_fusion.1), kind=kLoop, calls=%fused_computation.7 | loop fusion | flops 58720256 | bytes 109051904 | tf_op jit(solution)/shard_map/convert.5
  1018.9 15.5 fusion.3
  1034.4 31.5 %convolution_bitcast_fusion = f32[2,2,64,512,128]{3,4,0,2,1:T(8,128)} fusion(bf16[1,64,512,128]{2,3,1,0:T(8,128)(2,1)} %fusion.3, bf16[1,64,512,128]{2,3,1,0:T(8,128)(2,1)} %get-tuple-element.5, bf16[1,512,512]{2,1,0:T(8,128)(2,1)S(1)} %get-tuple-element.18, bf16[1,512,512]{2,1,0:T(8,128)(2,1)S(1)} %get-tuple-element.19), kind=kOutput, calls=%fused_computation | convolution fusion | flops 17215520768 | bytes 84934656 | tf_op jit(solution)/shard_map/tbd,scdk->tscbk/dot_general | solution.py:90
  1065.9 26.6 %subtract_convert_fusion = (bf16[1,64,512,128]{2,3,1,0:T(8,128)(2,1)S(1)}, bf16[1,64,512,128]{2,3,1,0:T(8,128)(2,1)}) fusion(f32[64,512]{1,0:T(8,128)S(1)} %get-tuple-element.17, f32[64,512]{1,0:T(8,128)S(1)} %get-tuple-element.16, f32[2,2,64,512,128]{3,4,0,2,1:T(8,128)} %convolution_bitcast_fusion), kind=kLoop, calls=%fused_computation.34 | loop fusion | flops 41943040 | bytes 84148224 | tf_op jit(solution)/shard_map/convert.3
  1103.0 22.7 %copy.78 = bf16[2,64,512,128]{3,1,0,2:T(8,128)(2,1)} copy(bf16[2,64,512,128]{2,3,1,0:T(8,128)(2,1)} %pad_maximum_fusion.1) | data formatting | bytes 33554432 | tf_op jit(solution)/shard_map/stack | solution.py:95
  1125.8 366.6 %all_to_all.75 = bf16[2,64,512,128]{3,1,0,2:T(8,128)(2,1)S(1)} all-to-all(bf16[2,64,512,128]{3,1,0,2:T(8,128)(2,1)} %copy.78), channel_id=1, replica_groups=mesh['seq'=16,'chan'=2] {'seq'}, dimensions={2} | all-to-all | bytes 33554432 | tf_op jit(solution)/shard_map/all_to_all | solution.py:98
  1492.4 36.1 %copy.79 = bf16[2,64,512,128]{3,2,1,0:T(8,128)(2,1)S(1)} copy(bf16[2,64,512,128]{3,1,0,2:T(8,128)(2,1)S(1)} %all_to_all.75) | data formatting | bytes 33554432 | tf_op jit(solution)/shard_map/all_to_all | solution.py:98
  1544.1 30.8 %fusion.26 = f32[1024,4096]{1,0:T(8,128)} fusion(bf16[128,8,32,128]{3,2,1,0:T(8,128)(2,1)} %bitcast.164), kind=kOutput, calls=%fused_computation.45 | convolution fusion | flops 8605663232 | bytes 25165824 | tf_op jit(solution)/shard_map/dot_general | solution.py:101
  1583.7 32.8 %fusion.18 = bf16[128,8,32,128]{3,1,2,0:T(8,128)(2,1)} fusion(f32[1024,4096]{1,0:T(8,128)} %fusion.26, bf16[128,8,32,128]{3,2,1,0:T(8,128)(2,1)} %bitcast.163), kind=kOutput, calls=%fused_computation.39 | convolution fusion | flops 8618246144 | bytes 33554432 | tf_op jit(solution)/shard_map/dot_general | solution.py:104
  1626.0 188.6 %all_to_all.76 = bf16[1024,32,128]{2,1,0:T(8,128)(2,1)} all-to-all(bf16[1024,32,128]{2,1,0:T(8,128)(2,1)} %bitcast.158), channel_id=1, replica_groups=mesh['seq'=16,'chan'=2] {'seq'}, dimensions={0} | all-to-all | bytes 16777216 | tf_op jit(solution)/shard_map/all_to_all | solution.py:109
  1826.1 15.2 fusion.15
  (22 shorter events, 122.4 us)
Async XLA Ops:
  12.2 188.9 %all-to-all-start = ((bf16[64,512,128]{2,0,1:T(8,128)(2,1)}), bf16[64,512,128]{2,0,1:T(8,128)(2,1)}, u32[]{:S(2)}, u32[]{:S(2)}) async-start(bf16[64,512,128]{2,0,1:T(8,128)(2,1)} %copy.61), calls=%async_computation | async-start | bytes 16777216 | tf_op jit(solution)/shard_map/all_to_all | solution.py:61
  201.0 366.9 %all-to-all-start.2 = ((bf16[2,32,1024,128]{3,1,0,2:T(8,128)(2,1)}), bf16[2,32,1024,128]{3,1,0,2:T(8,128)(2,1)}, u32[]{:S(2)}, u32[]{:S(2)}) async-start(bf16[2,32,1024,128]{3,1,0,2:T(8,128)(2,1)} %copy.71), calls=%async_computation.2 | async-start | bytes 33554432 | tf_op jit(solution)/shard_map/all_to_all | solution.py:88
  263.5 30.3 %copy-start = (bf16[4096,1024]{1,0:T(8,128)(2,1)S(1)}, bf16[4096,1024]{1,0:T(8,128)(2,1)}, u32[]{:S(2)}) copy-start(bf16[4096,1024]{1,0:T(8,128)(2,1)} %copy.64) | copy-start | bytes 25165828
  567.9 367.1 %all-to-all-start.1 = ((bf16[2,1024,32,128]{3,2,0,1:T(8,128)(2,1)}), bf16[2,1024,32,128]{3,2,0,1:T(8,128)(2,1)}, u32[]{:S(2)}, u32[]{:S(2)}) async-start(bf16[2,1024,32,128]{3,2,0,1:T(8,128)(2,1)} %copy.65), calls=%async_computation.1 | async-start | bytes 33554432 | tf_op jit(solution)/shard_map/all_to_all | solution.py:79
  1814.6 11.6 copy-start.1
where the time goes:
time: 1850 us; the launch traced here: 1840 us
  waiting for transfers between devices  687 us (37%)
  blocking collectives  555 us (30%)
  local copies, waits for them, and re-layouts  273 us (15%)
  matrix products  176 us (10%)
  other arithmetic  132 us (7%)
    all_to_all x1, blocking collectives, local(): lax.all_to_all(rotated, 'seq', split_axis=2, concat_axis=1, tiled=True)  367 us
    all_to_all x1, waiting for transfers between devices, local(): lax.all_to_all(columns, 'seq', split_axis=1, concat_axis=2, tiled=True)  315 us
    all_to_all x1, waiting for transfers between devices, local(): lax.all_to_all(filter_spectrum, 'seq', split_axis=2, concat_axis=1, tiled...  208 us
    all_to_all x1, blocking collectives, local(): lax.all_to_all(by_columns, 'seq', split_axis=0, concat_axis=1, tiled=True)  189 us
    all_to_all x1, waiting for transfers between devices, local(): lax.all_to_all(signal_grid, 'seq', split_axis=1, concat_axis=0, tiled=True)  164 us
    another operation x3, other arithmetic  79 us
    unnamed x7, local copies, waits for them, and re-layouts  43.3 us
    all_to_all x2, local copies, waits for them, and re-layouts, local(): lax.all_to_all(filter_spectrum, 'seq', split_axis=2, concat_axis=1, tiled...  41.7 us
  transfers between devices with their start and end apart: 3, of which 3 were waited for; matrix products, arithmetic and copies ran while one was open for 12% of the time, Pallas kernels for 0%

commit v1 on v0

v1 whole, which is shorter than its diff:
```python
import functools
import math

import jax
import jax.numpy as jnp
from jax import lax
from jax.experimental import pallas as pl
from jax.experimental.pallas import tpu as pltpu
from jax.sharding import PartitionSpec as P

OUTER = 1024
INNER = 512
SEQ = 524288
MESH = pl.DeviceIdType.MESH


def tables(length):
    indices = lax.iota(jnp.int32, length)
    angles = (
        2.0 * math.pi / length * (indices[:, None] * indices[None, :] % length).astype(jnp.float32)
    )
    return (jnp.cos(angles).astype(jnp.bfloat16), jnp.sin(angles).astype(jnp.bfloat16))


def twiddle(c_values, b_values, length):
    angles = (
        2.0
        * math.pi
        / length
        * (c_values[:, None] * b_values[None, :] % length).astype(jnp.float32)
    )
    return (jnp.cos(angles), jnp.sin(angles))


def exchange(arrays, out_shape, moves, shards, collective_id):
    count = len(moves)

    def kernel(*refs):
        ins, out = refs[: len(arrays)], refs[len(arrays)]
        send_sem, recv_sem, own_sem = refs[len(arrays) + 1 :]
        me = lax.axis_index("seq")
        barrier = pltpu.get_barrier_semaphore()
        for i in range(1, shards):
            pl.semaphore_signal(
                barrier, inc=1, device_id={"seq": lax.rem(me + i, shards)}, device_id_type=MESH
            )
        pl.semaphore_wait(barrier, shards - 1)
        copies = []
        for i in range(1, shards):
            to = lax.rem(me + i, shards)
            for m, (which, take, put) in enumerate(moves):
                copies.append(
                    pltpu.make_async_remote_copy(
                        src_ref=ins[which].at[take(to)],
                        dst_ref=out.at[put(me)],
                        send_sem=send_sem.at[(i - 1) * count + m],
                        recv_sem=recv_sem.at[(i - 1) * count + m],
                        device_id={"seq": to},
                        device_id_type=MESH,
                    )
                )
                copies[-1].start()
        for m, (which, take, put) in enumerate(moves):
            copies.append(
                pltpu.make_async_copy(ins[which].at[take(me)], out.at[put(me)], own_sem.at[m])
            )
            copies[-1].start()
        for copy in copies:
            copy.wait()

    return pl.pallas_call(
        kernel,
        out_shape=jax.ShapeDtypeStruct(out_shape, jnp.bfloat16),
        in_specs=[pl.BlockSpec(memory_space=pl.ANY)] * len(arrays),
        out_specs=pl.BlockSpec(memory_space=pl.ANY),
        scratch_shapes=[
            pltpu.SemaphoreType.DMA(((shards - 1) * count,)),
            pltpu.SemaphoreType.DMA(((shards - 1) * count,)),
            pltpu.SemaphoreType.DMA((count,)),
        ],
        compiler_params=pltpu.CompilerParams(collective_id=collective_id, has_side_effects=True),
        name=f"exchange_{collective_id}",
    )(*arrays)


def block(index, size, base=0):
    return pl.ds(pl.multiple_of(base + index * size, math.gcd(base, size) if base else size), size)


def section_kernel(fwd_ref, inv_ref, q_ref, filter_ref, cos_ref, sin_ref, out_ref):
    group = q_ref.shape[0]
    half = q_ref.shape[1] // 2
    scale = 1.0 / math.sqrt(half)
    lanes = q_ref.shape[2]
    q = jnp.concatenate([q_ref[g] for g in range(group)], axis=-1)
    spectrum = jnp.dot(fwd_ref[...], q, preferred_element_type=jnp.float32)
    spectrum = (spectrum * scale).astype(jnp.bfloat16).astype(jnp.float32)
    spec_re, spec_im = spectrum[:half], spectrum[half:]
    filt = jnp.concatenate([filter_ref[g] for g in range(group)], axis=-1).astype(jnp.float32)
    filter_re, filter_im = filt[:half], filt[half:]
    product = jnp.concatenate(
        [spec_re * filter_re - spec_im * filter_im, spec_re * filter_im + spec_im * filter_re],
        axis=0,
    ).astype(jnp.bfloat16)
    back = jnp.dot(inv_ref[...], product, preferred_element_type=jnp.float32) * scale
    back_re, back_im = back[:half], back[half:]
    for g in range(group):
        cols = slice(g * lanes, (g + 1) * lanes)
        re, im = back_re[:, cols], back_im[:, cols]
        cos, sin = cos_ref[g], sin_ref[g]
        out_ref[g, :half] = (re * cos - im * sin).astype(jnp.bfloat16)
        out_ref[g, half:] = (re * sin + im * cos).astype(jnp.bfloat16)


def section(fwd, inv, q, filt, cos, sin):
    rows, depth, lanes = q.shape
    group = 2
    whole = pl.BlockSpec((depth, depth), lambda i: (0, 0))
    full = pl.BlockSpec((group, depth, lanes), lambda i: (i, 0, 0))
    part = pl.BlockSpec((group, depth // 2, lanes), lambda i: (i, 0, 0))
    return pl.pallas_call(
        section_kernel,
        grid=(pl.cdiv(rows, group),),
        in_specs=[whole, whole, full, full, part, part],
        out_specs=full,
        out_shape=jax.ShapeDtypeStruct(q.shape, jnp.bfloat16),
        compiler_params=pltpu.CompilerParams(vmem_limit_bytes=56 * 1024 * 1024),
        name="section",
    )(fwd, inv, q, filt, cos, sin)


def local(signal, gate_values, skip_gain, filter_spectrum):
    shards = lax.axis_size("seq")
    own_index = lax.axis_index("seq")
    channels = signal.shape[1]
    outer_loc = OUTER // shards
    inner_loc = INNER // shards
    c_loc = -(-(OUTER // 2 + 1) // shards)
    rows = c_loc * shards
    cos_a, sin_a = tables(OUTER)
    cos_b, sin_b = tables(INNER)
    outer_scale = 1.0 / math.sqrt(OUTER)
    fwd_b = jnp.concatenate(
        [jnp.concatenate([cos_b, sin_b], 1), jnp.concatenate([-sin_b, cos_b], 1)], 0
    )
    inv_b = jnp.concatenate(
        [jnp.concatenate([cos_b, -sin_b], 1), jnp.concatenate([sin_b, cos_b], 1)], 0
    )
    own_b = own_index * inner_loc + lax.iota(jnp.int32, inner_loc)
    own_c = own_index * c_loc + lax.iota(jnp.int32, c_loc)
    c_all = lax.iota(jnp.int32, rows)
    cols_cos, cols_sin = twiddle(c_all, own_b, SEQ)
    rows_cos, rows_sin = twiddle(own_c, lax.iota(jnp.int32, INNER), SEQ)
    cols_cos = cols_cos[:, :, None]
    cols_sin = cols_sin[:, :, None]
    spread = (c_loc, INNER, channels)
    rows_cos = jnp.broadcast_to(rows_cos[:, :, None], spread)
    rows_sin = jnp.broadcast_to(rows_sin[:, :, None], spread)
    every = slice(None)

    def lead(size, base=0):
        return lambda t: (block(t, size, base), every, every)

    def middle(size, base=0):
        return lambda t: (every, block(t, size, base), every)

    signal_grid = signal.reshape(outer_loc, INNER, channels)
    pieces = exchange(
        [signal_grid],
        (OUTER, inner_loc, channels),
        [(0, middle(inner_loc), lead(outer_loc))],
        shards,
        0,
    )
    filter_rows = jnp.swapaxes(filter_spectrum[:, :, :rows], 1, 2)
    filter_cols = exchange(
        [filter_rows[0], filter_rows[1]],
        (c_loc, 2 * INNER, channels),
        [
            (0, lead(c_loc), middle(inner_loc)),
            (1, lead(c_loc), middle(inner_loc, INNER)),
        ],
        shards,
        1,
    )
    flattened = pieces.reshape(OUTER, inner_loc * channels)
    shape = (rows, inner_loc, channels)
    fwd_re = jnp.dot(cos_a[:rows], flattened, preferred_element_type=jnp.float32).reshape(shape)
    fwd_im = -jnp.dot(sin_a[:rows], flattened, preferred_element_type=jnp.float32).reshape(shape)
    q_re = ((fwd_re * cols_cos + fwd_im * cols_sin) * outer_scale).astype(jnp.bfloat16)
    q_im = ((fwd_im * cols_cos - fwd_re * cols_sin) * outer_scale).astype(jnp.bfloat16)
    q = exchange(
        [q_re, q_im],
        (c_loc, 2 * INNER, channels),
        [
            (0, lead(c_loc), middle(inner_loc)),
            (1, lead(c_loc), middle(inner_loc, INNER)),
        ],
        shards,
        2,
    )
    rotated = section(fwd_b, inv_b, q, filter_cols, rows_cos, rows_sin)
    pieces = exchange(
        [rotated],
        (2 * rows, inner_loc, channels),
        [
            (0, middle(inner_loc), lead(c_loc)),
            (0, middle(inner_loc, INNER), lead(c_loc, rows)),
        ],
        shards,
        3,
    )
    weight = jnp.where((c_all == 0) | (c_all == OUTER // 2), 1.0, 2.0)
    weight = jnp.where(c_all > OUTER // 2, 0.0, weight).astype(jnp.bfloat16)[None, :]
    back_a = jnp.concatenate([cos_a[:, :rows] * weight, -sin_a[:, :rows] * weight], 1)
    convolved = (
        jnp.dot(
            back_a,
            pieces.reshape(2 * rows, inner_loc * channels),
            preferred_element_type=jnp.float32,
        )
        * outer_scale
    )
    by_columns = convolved.astype(jnp.bfloat16).reshape(OUTER, inner_loc, channels)
    convolved = exchange(
        [by_columns],
        (outer_loc, INNER, channels),
        [(0, lead(outer_loc), middle(inner_loc))],
        shards,
        4,
    ).reshape(outer_loc * INNER, channels)
    result = gate_values.astype(jnp.float32) * (
        convolved.astype(jnp.float32) + skip_gain[None, :] * signal.astype(jnp.float32)
    )
    return result.astype(jnp.bfloat16)


def solution(mesh):
    return jax.shard_map(
        local,
        mesh=mesh,
        in_specs=(P("seq", "chan"), P("seq", "chan"), P("chan"), P(None, "seq", None, "chan")),
        out_specs=P("seq", "chan"),
        check_vma=False,
    )
```

time: 1850 us -> 1170 us (0.63)
  Pallas kernels: 0 us -> 988 us
  waiting for transfers between devices: 687 us -> 0 us
  blocking collectives: 555 us -> 0 us
  local copies, waits for them, and re-layouts: 273 us -> 70.2 us
  matrix products: 176 us -> 32.1 us
  other arithmetic: 132 us -> 67 us
    pallas_call x0 -> x6, Pallas kernels: none -> 988 us  [the longest x5 942 us: exchange(): pl.pallas_call(kernel, out_shape=jax.ShapeDtypeStruct(out_shape, jnp.bflo...]
    all_to_all x3 -> x0, waiting for transfers between devices: 687 us -> none  [the longest x1 315 us: local(): lax.all_to_all(columns, 'seq', split_axis=1, concat_axis=2, tiled=True)]
    all_to_all x2 -> x0, blocking collectives: 555 us -> none  [the longest x1 367 us: local(): lax.all_to_all(rotated, 'seq', split_axis=2, concat_axis=1, tiled=True)]
    dot_general x6 -> x3, matrix products: 176 us -> 32.1 us  [the longest x1 19.3 us: local(): jnp.dot(back_a, pieces.reshape(2 * rows, inner_loc * channels), preferred...]
    all_to_all x5 -> x0, local copies, waits for them, and re-layouts: 107 us -> none  [the longest x2 41.7 us: local(): lax.all_to_all(filter_spectrum, 'seq', split_axis=2, concat_axis=1, tiled...]
    another operation x5 -> x0, other arithmetic: 95.7 us -> none
    another operation x2 -> x0, local copies, waits for them, and re-layouts: 63 us -> none  [the longest x1 40.3 us: local(): jnp.stack([(fwd_re * cols_cos + fwd_im * cols_sin) * outer_scale, (fwd_im...]
    unnamed x7 -> x13, local copies, waits for them, and re-layouts: 43.3 us -> 35.1 us
  transfers between devices with their start and end apart: 3 -> 0, of which waited for: 3 -> 0; matrix products, arithmetic and copies ran while one was open for 12% -> 0% of each run, Pallas kernels for 0% -> 0%
where the time goes in v1:
time: 1170 us; the launch traced here: 1160 us
  Pallas kernels  988 us (84%)
  local copies, waits for them, and re-layouts  70.2 us (6%)
  other arithmetic  67 us (6%)
  matrix products  32.1 us (3%)
    pallas_call x5, Pallas kernels, exchange(): pl.pallas_call(kernel, out_shape=jax.ShapeDtypeStruct(out_shape, jnp.bflo...  942 us
    pallas_call x1, Pallas kernels, section(): pl.pallas_call(section_kernel, grid=(pl.cdiv(rows, group),), in_specs=[wh...  46.5 us
    unnamed x13, local copies, waits for them, and re-layouts  35.1 us

profile of v1, /device:TPU:11, one launch (start us, length us, event | category | flops | bytes accessed | tf_op | source)
XLA Modules:
  0.0 1158.0 jit_solution(6289874461502434364)
XLA Ops:
  0.4 4.0 fusion.33
  5.5 4.3 sine_convert_fusion.1
  9.8 10.1 fusion.17
  20.0 17.1 %sine_convert_fusion = (bf16[1024,1024]{1,0:T(8,128)(2,1)S(1)}, bf16[1024,1024]{1,0:T(8,128)(2,1)S(1)}) fusion(), kind=kLoop, calls=%fused_computation.20 | loop fusion | flops 16777216 | bytes 4194304 | tf_op jit(solution)/shard_map/convert_element_type | solution.py:22
  38.4 1.7 slice_multiply_fusion
  40.1 185.4 %exchange_0.1 = bf16[1024,32,128]{2,1,0:T(8,128)(2,1)} custom-call(bf16[64,512,128]{2,1,0:T(8,128)(2,1)} %bitcast.37), custom_call_target="tpu_custom_call" | custom-call | tf_op jit(solution)/shard_map/exchange_0/pallas_call | solution.py:71
  225.6 15.3 %copy.30 = bf16[128,8,32,128]{3,1,2,0:T(8,128)(2,1)} copy(bf16[128,8,32,128]{3,2,1,0:T(8,128)(2,1)} %bitcast.40) | data formatting | bytes 16777216
  240.8 12.0 %copy.5 = bf16[4096,1024]{1,0:T(8,128)(2,1)} copy(bf16[4096,1024]{0,1:T(8,128)(2,1)} %bitcast.38) | data formatting | bytes 16777216 | tf_op jit(solution)/shard_map/dot_general | solution.py:188
  252.9 8.1 fusion.19
  261.0 4.7 fusion.20
  265.7 15.9 %multiply_convert_fusion.1 = (bf16[528,32,128]{2,1,0:T(8,128)(2,1)}, bf16[528,32,128]{2,1,0:T(8,128)(2,1)}) fusion(f32[528,32,128]{2,0,1:T(8,128)S(1)} %fusion.20, f32[528,32,128]{2,0,1:T(8,128)S(1)} %fusion.19, f32[528,32]{1,0:T(8,128)S(1)} %get-tuple-element.16, f32[528,32]{1,0:T(8,128)S(1)} %get-tuple-element.15), kind=kLoop, calls=%fused_computation.8 | loop fusion | flops 23789568 | bytes 26087424 | tf_op jit(solution)/shard_map/convert_element_type | solution.py:191
  281.6 190.5 %exchange_2.1.q_ref = bf16[33,1024,128]{2,1,0:T(8,128)(2,1)} custom-call(bf16[528,32,128]{2,1,0:T(8,128)(2,1)} %get-tuple-element.6.refs_0_, bf16[528,32,128]{2,1,0:T(8,128)(2,1)} %get-tuple-element.5.refs_1_), custom_call_target="tpu_custom_call" | custom-call | tf_op jit(solution)/shard_map/exchange_2/pallas_call | solution.py:71
  472.1 4.6 broadcast_in_dim.17.sin_ref
  476.7 4.6 broadcast_in_dim.16.cos_ref
  481.3 7.4 slice.25
  488.7 9.0 copy.29
  497.8 6.4 slice_bitcast_fusion
  504.2 190.5 %exchange_1.1.filter_ref = bf16[33,1024,128]{2,1,0:T(8,128)(2,1)} custom-call(bf16[528,32,128]{2,1,0:T(8,128)(2,1)} %get-tuple-element.8.refs_0_, bf16[528,32,128]{2,1,0:T(8,128)(2,1)} %get-tuple-element.7.refs_1_), custom_call_target="tpu_custom_call" | custom-call | tf_op jit(solution)/shard_map/exchange_1/pallas_call | solution.py:71
  694.7 46.5 %section.1.refs_0_ = bf16[33,1024,128]{2,1,0:T(8,128)(2,1)} custom-call(bf16[1024,1024]{1,0:T(8,128)(2,1)} %get-tuple-element.10.fwd_ref, bf16[1024,1024]{1,0:T(8,128)(2,1)} %get-tuple-element.9.inv_ref, bf16[33,1024,128]{2,1,0:T(8,128)(2,1)} %exchange_2.1.q_ref, bf16[33,1024,128]{2,1,0:T(8,128)(2,1)} %exchange_1.1.filter_ref, ...), custom_call_target="tpu_custom_call" | custom-call | tf_op jit(solution)/shard_map/section/pallas_call | solution.py:121
  741.3 190.6 %exchange_3.1 = bf16[1056,32,128]{2,1,0:T(8,128)(2,1)} custom-call(bf16[33,1024,128]{2,1,0:T(8,128)(2,1)} %section.1.refs_0_), custom_call_target="tpu_custom_call" | custom-call | tf_op jit(solution)/shard_map/exchange_3/pallas_call | solution.py:71
  931.9 19.3 %fusion.4 = bf16[128,8,32,128]{3,1,2,0:T(8,128)(2,1)} fusion(bf16[132,8,32,128]{3,2,1,0:T(8,128)(2,1)} %bitcast.41, bf16[1024,528]{1,0:T(8,128)(2,1)S(1)} %copy-done.3, bf16[1024,528]{1,0:T(8,128)(2,1)S(1)} %copy-done.2), kind=kOutput, calls=%fused_computation.14 | convolution fusion | flops 8871084032 | bytes 19202048 | tf_op jit(solution)/shard_map/dot_general | solution.py:217
  951.2 9.4 copy.13
  960.6 184.6 %exchange_4.1 = bf16[64,512,128]{2,1,0:T(8,128)(2,1)} custom-call(bf16[1024,32,128]{2,1,0:T(8,128)(2,1)} %bitcast.39), custom_call_target="tpu_custom_call" | custom-call | tf_op jit(solution)/shard_map/exchange_4/pallas_call | solution.py:71
  1145.2 12.3 %fusion.1 = bf16[32768,128]{1,0:T(8,128)(2,1)} fusion(bf16[32768,128]{1,0:T(8,128)(2,1)} %param.4, bf16[32768,128]{1,0:T(8,128)(2,1)} %param.5, bf16[64,512,128]{2,1,0:T(8,128)(2,1)} %exchange_4.1, f32[128]{0:T(128)S(1)} %copy-done.4), kind=kLoop, calls=%fused_computation.2 | loop fusion | flops 29360128 | bytes 33554944 | tf_op jit(solution)/shard_map/convert_element_type | solution.py:235
  (15 shorter events, 2.9 us)
Async XLA Ops:
  37.0 1.4 copy-start.1
  252.8 8.1 copy-start
  741.2 190.6 %copy-start.2 = (bf16[1024,528]{1,0:T(8,128)(2,1)S(1)}, bf16[1024,528]{1,0:T(8,128)(2,1)}, u32[]{:S(2)}) copy-start(bf16[1024,528]{1,0:T(8,128)(2,1)} %get-tuple-element.11) | copy-start | bytes 3244036
  741.3 190.6 %copy-start.3 = (bf16[1024,528]{1,0:T(8,128)(2,1)S(1)}, bf16[1024,528]{1,0:T(8,128)(2,1)}, u32[]{:S(2)}) copy-start(bf16[1024,528]{1,0:T(8,128)(2,1)} %get-tuple-element.12) | copy-start | bytes 3244036
  960.6 184.6 %copy-start.4 = (f32[128]{0:T(128)S(1)}, f32[128]{0:T(128)}, u32[]{:S(2)}) copy-start(f32[128]{0:T(128)} %param.6) | copy-start | bytes 1540

commit v2 on v1

v2 whole, which is shorter than its diff:
```python
import functools
import math

import jax
import jax.numpy as jnp
from jax import lax
from jax.experimental import pallas as pl
from jax.experimental.pallas import tpu as pltpu
from jax.sharding import PartitionSpec as P

OUTER = 1024
INNER = 512
SEQ = 524288
MESH = pl.DeviceIdType.MESH


def tables(length):
    indices = lax.iota(jnp.int32, length)
    angles = (
        2.0 * math.pi / length * (indices[:, None] * indices[None, :] % length).astype(jnp.float32)
    )
    return (jnp.cos(angles).astype(jnp.bfloat16), jnp.sin(angles).astype(jnp.bfloat16))


def twiddle(c_values, b_values, length):
    angles = (
        2.0
        * math.pi
        / length
        * (c_values[:, None] * b_values[None, :] % length).astype(jnp.float32)
    )
    return (jnp.cos(angles), jnp.sin(angles))


def exchange(arrays, out_shape, moves, shards, collective_id):
    count = len(moves)

    def kernel(*refs):
        ins, out = refs[: len(arrays)], refs[len(arrays)]
        send_sem, recv_sem, own_sem = refs[len(arrays) + 1 :]
        me = lax.axis_index("seq")
        barrier = pltpu.get_barrier_semaphore()
        for i in range(1, shards):
            pl.semaphore_signal(
                barrier, inc=1, device_id={"seq": lax.rem(me + i, shards)}, device_id_type=MESH
            )
        pl.semaphore_wait(barrier, shards - 1)
        copies = []
        for i in range(1, shards):
            to = lax.rem(me + i, shards)
            for m, (which, take, put) in enumerate(moves):
                copies.append(
                    pltpu.make_async_remote_copy(
                        src_ref=ins[which].at[take(to)],
                        dst_ref=out.at[put(me)],
                        send_sem=send_sem.at[(i - 1) * count + m],
                        recv_sem=recv_sem.at[(i - 1) * count + m],
                        device_id={"seq": to},
                        device_id_type=MESH,
                    )
                )
                copies[-1].start()
        for m, (which, take, put) in enumerate(moves):
            copies.append(
                pltpu.make_async_copy(ins[which].at[take(me)], out.at[put(me)], own_sem.at[m])
            )
            copies[-1].start()
        for copy in copies:
            copy.wait()

    return pl.pallas_call(
        kernel,
        out_shape=jax.ShapeDtypeStruct(out_shape, jnp.bfloat16),
        in_specs=[pl.BlockSpec(memory_space=pl.ANY)] * len(arrays),
        out_specs=pl.BlockSpec(memory_space=pl.ANY),
        scratch_shapes=[
            pltpu.SemaphoreType.DMA(((shards - 1) * count,)),
            pltpu.SemaphoreType.DMA(((shards - 1) * count,)),
            pltpu.SemaphoreType.DMA((count,)),
        ],
        compiler_params=pltpu.CompilerParams(collective_id=collective_id, has_side_effects=True),
        name=f"exchange_{collective_id}",
    )(*arrays)


def block(index, size, base=0):
    return pl.ds(pl.multiple_of(base + index * size, math.gcd(base, size) if base else size), size)


def local(signal, gate_values, skip_gain, filter_spectrum):
    shards = lax.axis_size("seq")
    channels = signal.shape[1]
    ch_loc = channels // shards
    outer_loc = OUTER // shards
    inner_loc = INNER // shards
    rows = -(-(OUTER // 2 + 1) // 16) * 16
    cos_a, sin_a = tables(OUTER)
    cos_b, sin_b = tables(INNER)
    outer_scale = 1.0 / math.sqrt(OUTER)
    inner_scale = 1.0 / math.sqrt(INNER)
    fwd_b = jnp.concatenate(
        [jnp.concatenate([cos_b, sin_b], 1), jnp.concatenate([-sin_b, cos_b], 1)], 0
    )
    inv_b = jnp.concatenate(
        [jnp.concatenate([cos_b, -sin_b], 1), jnp.concatenate([sin_b, cos_b], 1)], 0
    )
    c_all = lax.iota(jnp.int32, rows)
    cos, sin = twiddle(lax.iota(jnp.int32, INNER), c_all, SEQ)
    every = slice(None)

    def lead(size):
        return lambda t: (block(t, size), every, every)

    def middle(size):
        return lambda t: (every, block(t, size), every)

    grid = exchange(
        [signal.T.reshape(channels, outer_loc, INNER)],
        (ch_loc, OUTER, INNER),
        [(0, lead(ch_loc), middle(outer_loc))],
        shards,
        0,
    )
    filt = [
        exchange(
            [filter_spectrum[p, :, :rows].transpose(2, 0, 1)],
            (ch_loc, INNER, rows),
            [(0, lead(ch_loc), middle(inner_loc))],
            shards,
            1 + p,
        ).astype(jnp.float32)
        for p in range(2)
    ]
    fwd_re = jnp.einsum(
        "kab,ac->kbc", grid, cos_a[:, :rows], preferred_element_type=jnp.float32
    )
    fwd_im = -jnp.einsum(
        "kab,ac->kbc", grid, sin_a[:, :rows], preferred_element_type=jnp.float32
    )
    q = jnp.concatenate(
        [
            (fwd_re * cos + fwd_im * sin) * outer_scale,
            (fwd_im * cos - fwd_re * sin) * outer_scale,
        ],
        axis=1,
    ).astype(jnp.bfloat16)
    spectrum = jnp.einsum("db,kbc->kdc", fwd_b, q, preferred_element_type=jnp.float32)
    spectrum = (spectrum * inner_scale).astype(jnp.bfloat16).astype(jnp.float32)
    re, im = spectrum[:, :INNER], spectrum[:, INNER:]
    product = jnp.concatenate(
        [re * filt[0] - im * filt[1], re * filt[1] + im * filt[0]], axis=1
    ).astype(jnp.bfloat16)
    back = jnp.einsum("bd,kdc->kbc", inv_b, product, preferred_element_type=jnp.float32)
    back = back * inner_scale
    re, im = back[:, :INNER], back[:, INNER:]
    r_re = (re * cos - im * sin).astype(jnp.bfloat16)
    r_im = (re * sin + im * cos).astype(jnp.bfloat16)
    weight = jnp.where((c_all == 0) | (c_all == OUTER // 2), 1.0, 2.0)
    weight = jnp.where(c_all > OUTER // 2, 0.0, weight).astype(jnp.bfloat16)[None, :]
    convolved = (
        jnp.einsum(
            "ac,kbc->kab", cos_a[:, :rows] * weight, r_re, preferred_element_type=jnp.float32
        )
        - jnp.einsum(
            "ac,kbc->kab", sin_a[:, :rows] * weight, r_im, preferred_element_type=jnp.float32
        )
    ) * outer_scale
    convolved = exchange(
        [convolved.astype(jnp.bfloat16)],
        (channels, outer_loc, INNER),
        [(0, middle(outer_loc), lead(ch_loc))],
        shards,
        3,
    )
    convolved = convolved.reshape(channels, outer_loc * INNER).T
    result = gate_values.astype(jnp.float32) * (
        convolved.astype(jnp.float32) + skip_gain[None, :] * signal.astype(jnp.float32)
    )
    return result.astype(jnp.bfloat16)


def solution(mesh):
    return jax.shard_map(
        local,
        mesh=mesh,
        in_specs=(P("seq", "chan"), P("seq", "chan"), P("chan"), P(None, "seq", None, "chan")),
        out_specs=P("seq", "chan"),
        check_vma=False,
    )
```

time: 1170 us -> 894 us (0.76)
  Pallas kernels: 988 us -> 604 us
  matrix products: 32.1 us -> 135 us
  other arithmetic: 67 us -> 83.6 us
    pallas_call x5 -> x4, Pallas kernels: 942 us -> 604 us  [exchange(): pl.pallas_call(kernel, out_shape=jax.ShapeDtypeStruct(out_shape, jnp.bflo...]
    dot_general x3 -> x6, matrix products: 32.1 us -> 135 us  [the longest x1 54.2 us: local(): jnp.einsum('db,kbc->kdc', fwd_b, q, preferred_element_type=jnp.float32)]
    pallas_call x1 -> x0, Pallas kernels: 46.5 us -> none  [section(): pl.pallas_call(section_kernel, grid=(pl.cdiv(rows, group),), in_specs=[wh...]
    another operation x0 -> x2, other arithmetic: none -> 30 us
    unnamed x13 -> x14, local copies, waits for them, and re-layouts: 35.1 us -> 17.8 us
    convert_element_type x2 -> x1, other arithmetic: 21.4 us -> 4.31 us  [tables(): jnp.sin(angles).astype(jnp.bfloat16)]
    concatenate x0 -> x1, local copies, waits for them, and re-layouts: none -> 15.2 us  [local(): jnp.concatenate([re * filt[0] - im * filt[1], re * filt[1] + im * filt[0]...]
    convert_element_type x0 -> x1, local copies, waits for them, and re-layouts: none -> 14.7 us  [local(): convolved.astype(jnp.float32)]
where the time goes in v2:
time: 894 us; the launch traced here: 891 us
  Pallas kernels  604 us (68%)
  matrix products  135 us (15%)
  other arithmetic  83.6 us (9%)
  local copies, waits for them, and re-layouts  66.6 us (7%)
    pallas_call x4, Pallas kernels, exchange(): pl.pallas_call(kernel, out_shape=jax.ShapeDtypeStruct(out_shape, jnp.bflo...  604 us
    dot_general x1, matrix products, local(): jnp.einsum('db,kbc->kdc', fwd_b, q, preferred_element_type=jnp.float32)  54.2 us
    another operation x2, other arithmetic  30 us
    dot_general x1, matrix products, local(): jnp.einsum('ac,kbc->kab', sin_a[:, :rows] * weight, r_im, preferred_eleme...  21.1 us
    dot_general x1, matrix products, local(): jnp.einsum('ac,kbc->kab', cos_a[:, :rows] * weight, r_re, preferred_eleme...  18.6 us

profile of v2, /device:TPU:11, one launch (start us, length us, event | category | flops | bytes accessed | tf_op | source)
XLA Modules:
  0.0 890.5 jit_solution(4025072793836846918)
XLA Ops:
  4.0 12.8 %copy.40.refs_0_ = bf16[128,64,512]{2,1,0:T(8,128)(2,1)} copy(bf16[128,64,512]{0,2,1:T(8,128)(2,1)} %bitcast.66) | data formatting | bytes 16777216 | tf_op jit(solution)/shard_map/reshape | solution.py:118
  16.8 185.6 %exchange_0.1 = bf16[8,1024,512]{2,1,0:T(8,128)(2,1)} custom-call(bf16[128,64,512]{2,1,0:T(8,128)(2,1)} %copy.40.refs_0_), custom_call_target="tpu_custom_call" | custom-call | tf_op jit(solution)/shard_map/exchange_0/pallas_call | solution.py:71
  202.4 15.2 %fusion.41 = f32[528,8,512]{2,0,1:T(8,128)S(1)} fusion(bf16[8,1024,512]{2,1,0:T(8,128)(2,1)} %exchange_0.1, f32[1024,1024]{0,1:T(8,128)} %fusion.22), kind=kOutput, calls=%fused_computation.70 | convolution fusion | flops 4429725696 | bytes 19202048 | tf_op jit(solution)/shard_map/kab,ac->kbc/dot_general | solution.py:137
  217.6 11.2 %fusion.43 = f32[528,8,512]{2,0,1:T(8,128)S(1)} fusion(bf16[8,1024,512]{2,1,0:T(8,128)(2,1)S(1)} %copy-done, f32[1024,1024]{0,1:T(8,128)S(1)} %copy-done.1), kind=kOutput, calls=%fused_computation.72 | convolution fusion | flops 4429725696 | bytes 19202048 | tf_op jit(solution)/shard_map/kab,ac->kbc/dot_general | solution.py:134
  228.8 4.2 fusion.58
  233.0 18.3 %fusion.8 = (bf16[8,512,528]{1,0,2:T(8,128)(2,1)}, bf16[8,512,528]{1,0,2:T(8,128)(2,1)}) fusion(f32[528,8,512]{2,0,1:T(8,128)S(1)} %fusion.43, f32[528,8,512]{2,0,1:T(8,128)S(1)} %fusion.41, f32[512,528]{0,1:T(8,128)S(1)} %get-tuple-element.13, f32[512,528]{0,1:T(8,128)S(1)} %get-tuple-element.14), kind=kLoop, calls=%fused_computation.21 | loop fusion | flops 23789568 | bytes 28114944 | tf_op jit(solution)/shard_map/convert.5
  251.3 8.1 pad_maximum_fusion.1
  259.4 4.3 sine_convert_fusion.1
  267.7 54.2 %convert_bitcast_fusion = f32[8,1024,528]{2,1,0:T(8,128)} fusion(bf16[8,1024,528]{1,0,2:T(8,128)(2,1)} %pad_maximum_fusion.1, bf16[512,512]{1,0:T(8,128)(2,1)S(1)} %get-tuple-element.16, bf16[512,512]{1,0:T(8,128)(2,1)S(1)} %fusion.60, bf16[512,512]{1,0:T(8,128)(2,1)S(1)} %get-tuple-element.15), kind=kOutput, calls=%fused_computation | convolution fusion | flops 8879734784 | bytes 27525120 | tf_op jit(solution)/shard_map/db,kbc->kdc/dot_general | solution.py:147
  322.0 6.2 fusion.64
  328.1 8.9 copy.43
  337.0 117.1 %exchange_1.1 = bf16[8,512,528]{2,1,0:T(8,128)(2,1)} custom-call(bf16[128,32,528]{2,1,0:T(8,128)(2,1)} %bitcast.67), custom_call_target="tpu_custom_call" | custom-call | tf_op jit(solution)/shard_map/exchange_1/pallas_call | solution.py:71
  454.1 8.9 copy.44
  463.0 117.2 %exchange_2.1 = bf16[8,512,528]{2,1,0:T(8,128)(2,1)} custom-call(bf16[128,32,528]{2,1,0:T(8,128)(2,1)} %bitcast.68), custom_call_target="tpu_custom_call" | custom-call | tf_op jit(solution)/shard_map/exchange_2/pallas_call | solution.py:71
  580.2 11.7 %fusion.3 = (bf16[8,512,528]{2,1,0:T(8,128)(2,1)S(1)}, bf16[8,512,528]{2,1,0:T(8,128)(2,1)S(1)}) fusion(bf16[8,512,528]{2,1,0:T(8,128)(2,1)} %exchange_1.1, bf16[8,512,528]{2,1,0:T(8,128)(2,1)} %exchange_2.1, f32[8,1024,528]{2,1,0:T(8,128)} %convert_bitcast_fusion), kind=kLoop, calls=%fused_computation.12 | loop fusion | flops 21626880 | bytes 34603008 | tf_op jit(solution)/shard_map/convert.3
  591.9 5.7 pad_maximum_fusion
  597.6 15.2 %copy.36 = bf16[8,1024,528]{1,0,2:T(8,128)(2,1)} copy(bf16[8,1024,528]{2,1,0:T(8,128)(2,1)} %pad_maximum_fusion) | data formatting | bytes 17301504 | tf_op jit(solution)/shard_map/concatenate | solution.py:150
  612.8 15.0 %multiply_bitcast_fusion = f32[8,1024,528]{1,0,2:T(8,128)} fusion(bf16[8,1024,528]{1,0,2:T(8,128)(2,1)} %copy.36, bf16[512,512]{1,0:T(8,128)(2,1)S(1)} %get-tuple-element.16, bf16[512,512]{1,0:T(8,128)(2,1)S(1)} %get-tuple-element.15, bf16[512,512]{1,0:T(8,128)(2,1)} %copy-done.4), kind=kOutput, calls=%fused_computation.2 | convolution fusion | flops 8871084032 | bytes 27525120 | tf_op jit(solution)/shard_map/bd,kdc->kbc/dot_general | solution.py:153
  627.8 8.1 add_convert_fusion
  635.9 18.6 %fusion.18 = f32[8,512,1024]{1,2,0:T(8,128)} fusion(bf16[8,512,528]{1,0,2:T(8,128)(2,1)S(1)} %get-tuple-element.8, bf16[528]{0:T(1024)(128)(2,1)S(1)} %select_convert_fusion, f32[1024,1024]{0,1:T(8,128)S(1)} %copy-done.2), kind=kOutput, calls=%fused_computation.37 | convolution fusion | flops 4431888384 | bytes 23267328 | tf_op jit(solution)/shard_map/ac,kbc->kab/dot_general | solution.py:161
  654.5 21.1 %fusion.16.refs_0_ = bf16[8,1024,512]{2,1,0:T(8,128)(2,1)} fusion(f32[8,512,1024]{1,2,0:T(8,128)} %fusion.18, bf16[8,512,528]{1,0,2:T(8,128)(2,1)S(1)} %get-tuple-element.7, bf16[528]{0:T(1024)(128)(2,1)S(1)} %select_convert_fusion, f32[1024,1024]{0,1:T(8,128)S(1)} %copy-done.3), kind=kOutput, calls=%fused_computation.35 | convolution fusion | flops 4444471296 | bytes 31655936 | tf_op jit(solution)/shard_map/ac,kbc->kab/dot_general | solution.py:164
  675.6 184.6 %exchange_3.1 = bf16[128,64,512]{2,1,0:T(8,128)(2,1)} custom-call(bf16[8,1024,512]{2,1,0:T(8,128)(2,1)} %fusion.16.refs_0_), custom_call_target="tpu_custom_call" | custom-call | tf_op jit(solution)/shard_map/exchange_3/pallas_call | solution.py:71
  860.2 14.7 %copy.42 = f32[128,64,512]{0,2,1:T(8,128)} copy(bf16[128,64,512]{2,1,0:T(8,128)(2,1)} %exchange_3.1) | data formatting | bytes 25165824 | tf_op jit(solution)/shard_map/convert_element_type | solution.py:177
  874.8 15.2 %fusion.1 = bf16[32768,128]{1,0:T(8,128)(2,1)} fusion(f32[128,64,512]{0,2,1:T(8,128)} %copy.42, bf16[32768,128]{1,0:T(8,128)(2,1)} %param.4, bf16[32768,128]{1,0:T(8,128)(2,1)} %param.5, f32[128]{0:T(128)S(1)} %copy-done.5), kind=kLoop, calls=%fused_computation.5 | loop fusion | flops 25165824 | bytes 41943552 | tf_op jit(solution)/shard_map/convert_element_type | solution.py:179
  (15 shorter events, 8.0 us)
Async XLA Ops:
  202.4 15.2 %copy-start = (bf16[8,1024,512]{2,1,0:T(8,128)(2,1)S(1)}, bf16[8,1024,512]{2,1,0:T(8,128)(2,1)}, u32[]{:S(2)}) copy-start(bf16[8,1024,512]{2,1,0:T(8,128)(2,1)} %exchange_0.1) | copy-start | bytes 25165828
  202.4 15.2 %copy-start.1 = (f32[1024,1024]{0,1:T(8,128)S(1)}, f32[1024,1024]{0,1:T(8,128)}, u32[]{:S(2)}) copy-start(f32[1024,1024]{0,1:T(8,128)} %fusion.22) | copy-start | bytes 12582916
  267.7 54.2 %copy-start.4 = (bf16[512,512]{1,0:T(8,128)(2,1)}, bf16[512,512]{1,0:T(8,128)(2,1)S(1)}, u32[]{:S(2)}) copy-start(bf16[512,512]{1,0:T(8,128)(2,1)S(1)} %fusion.60) | copy-start | bytes 1572868
  627.8 8.1 copy-start.2
  635.9 18.6 %copy-start.3 = (f32[1024,1024]{0,1:T(8,128)S(1)}, f32[1024,1024]{0,1:T(8,128)}, u32[]{:S(2)}) copy-start(f32[1024,1024]{0,1:T(8,128)} %fusion.22) | copy-start | bytes 12582916
  860.2 14.7 %copy-start.5 = (f32[128]{0:T(128)S(1)}, f32[128]{0:T(128)}, u32[]{:S(2)}) copy-start(f32[128]{0:T(128)} %param.6) | copy-start | bytes 1540
